TPU v7x, 32 devices: a whole 2x2x4 slice. The times are simulated.
32 devices in a mesh: freq: 8 (over z, x), kgrp: 4 (over y, core).
Axes of the slice: x: 2, y: 2, z: 4, core: 2. Of those that a mesh axis runs over, the one named last changes fastest.
Arguments:
- hamiltonian: float32 [256, 64, 128], P(('freq', 'kgrp')), may hold values from -1 to 1, as said below
- self_energy: float32 [16, 64, 128], P('freq'), may hold values from -0.8 to 0.3, as said below
- guess_factor: float32 [16, 64, 128], P('freq'), may hold values from -0.05 to 1.25
- weights: int32 [256], replicated, may hold values from 1 to 48
- counts: int32 [16], replicated, may hold values from 1 to 3, as said below
Outputs:
- local_green: float32 [4096, 32], P(('freq', 'kgrp'))
Inputs may be any that keep to these rules, and one draw needn't show every extreme that they name: `hamiltonian`: each k-point's matrix is Hermitian: the left half symmetric, the right half antisymmetric. `self_energy`: the diagonal of the right half lies between -0.8 and -0.4. `counts`: the number of Newton-Schulz steps taken at each frequency.
All inputs are finite; a program needn't handle non-finite values.
Results may differ from a plain program's by a relative error of at most 0.0001.
Values sent between devices are 32-bit elements.
A program may use at most 64 MiB of HBM per device.

v0:
```python
import math

import jax
import jax.numpy as jnp
from jax import lax
from jax.sharding import PartitionSpec as P

chem_potential = 0.2


def blockify(right_side):
    order = right_side.shape[-1] // 2
    real_part = right_side[..., :order]
    imag_part = right_side[..., order:]
    upper_row = jnp.concatenate([real_part, imag_part], -1)
    lower_row = jnp.concatenate([-imag_part, real_part], -1)
    return jnp.concatenate([upper_row, lower_row], -2)


def complex_product(left_side, right_side):
    return jnp.einsum(
        "...ij,...jl->...il", left_side, blockify(right_side), precision=lax.Precision.HIGHEST
    )


def build_matrix(kpoint_rows, sigma_rows, matsubara):
    orbitals = kpoint_rows.shape[1]
    identity = jnp.eye(orbitals, dtype=jnp.float32)
    real_shift = jnp.broadcast_to(chem_potential * identity, matsubara.shape + identity.shape)
    imag_shift = matsubara[:, None, None] * identity
    diagonal_shift = jnp.concatenate([real_shift, imag_shift], -1)
    return diagonal_shift[:, None] - kpoint_rows[None] - sigma_rows[:, None]


def start_guess(matrix, factor_rows):
    orbitals = matrix.shape[-2]
    diag_real = jnp.diagonal(matrix[..., :orbitals], axis1=-2, axis2=-1)
    diag_imag = jnp.diagonal(matrix[..., orbitals:], axis1=-2, axis2=-1)
    modulus = diag_real * diag_real + diag_imag * diag_imag
    recip_real = (diag_real / modulus)[..., None]
    recip_imag = (-diag_imag / modulus)[..., None]
    factor_real = factor_rows[..., :orbitals]
    factor_imag = factor_rows[..., orbitals:]
    guess_real = recip_real * factor_real - recip_imag * factor_imag
    guess_imag = recip_real * factor_imag + recip_imag * factor_real
    return jnp.concatenate([guess_real, guess_imag], -1)


def invert_blocks(kpoint_rows, sigma_rows, factor_rows, freq_ids, freq_total, step_counts):
    orbitals = kpoint_rows.shape[1]
    matsubara = (2 * freq_ids + 1).astype(jnp.float32) * (math.pi / (2 * freq_total))
    matrix = build_matrix(kpoint_rows, sigma_rows, matsubara)
    initial = start_guess(matrix, factor_rows[:, None])
    identity = jnp.eye(orbitals, dtype=jnp.float32)
    doubled = jnp.concatenate([2.0 * identity, jnp.zeros_like(identity)], -1)
    longest = jnp.max(step_counts)

    def newton_step(sweep, current):
        updated = complex_product(current, doubled - complex_product(matrix, current))
        active = (sweep < step_counts)[:, None, None, None]
        return jnp.where(active, updated, current)

    return lax.fori_loop(0, longest, newton_step, initial)


def per_device(hamiltonian, self_energy, guess_factor, weights, counts):
    orbitals = hamiltonian.shape[1]
    per_freq = self_energy.shape[0]
    k_local = hamiltonian.shape[0]
    freq_devs = lax.axis_size("freq")
    group_devs = lax.axis_size("kgrp")
    freq_total = per_freq * freq_devs
    pair_block = orbitals * orbitals // (freq_devs * group_devs)
    freq_pos = lax.axis_index("freq")
    group_pos = lax.axis_index("kgrp")
    weight_total = jnp.sum(weights.astype(jnp.float32))
    first_freq = freq_pos * per_freq
    freq_ids = first_freq + jnp.arange(per_freq, dtype=jnp.int32)
    local_counts = lax.dynamic_slice_in_dim(counts, first_freq, per_freq)
    empty = jnp.zeros((per_freq, orbitals, 2 * orbitals), jnp.float32)
    h_piece = lax.all_gather(hamiltonian, "freq", axis=0, tiled=True)
    row_ids = jnp.arange(h_piece.shape[0], dtype=jnp.int32)
    kpoint_ids = (
        row_ids // k_local * (group_devs * k_local) + group_pos * k_local + row_ids % k_local
    )
    factors = jnp.take(weights, kpoint_ids).astype(jnp.float32)
    inverses = invert_blocks(h_piece, self_energy, guess_factor, freq_ids, freq_total, local_counts)
    partial_sum = empty + jnp.einsum(
        "k,fkij->fij", factors, inverses, precision=lax.Precision.HIGHEST
    )
    partial_term = partial_sum.reshape(per_freq, orbitals, 2, orbitals).transpose(0, 2, 1, 3)
    partial_term = partial_term.reshape(per_freq, 2, freq_devs, group_devs, pair_block)
    quarter = lax.psum_scatter(partial_term, "kgrp", scatter_dimension=3, tiled=True)
    own_block = lax.all_to_all(quarter, "freq", split_axis=2, concat_axis=0, tiled=True)
    result = own_block.reshape(freq_total, 2, pair_block).transpose(2, 1, 0)
    result = result.reshape(pair_block, 2 * freq_total)
    return result / weight_total


def solution(mesh):
    return jax.shard_map(
        per_device,
        mesh=mesh,
        in_specs=(
            P(("freq", "kgrp"), None, None),
            P("freq", None, None),
            P("freq", None, None),
            P(),
            P(),
        ),
        out_specs=P(("freq", "kgrp"), None),
        check_vma=False,
    )
```

profile of v0, /device:TPU:0, one launch (start us, length us, event | category | flops | bytes accessed | tf_op | source)
XLA Modules:
  0.0 254.6 jit_solution(18190789245727477502)
XLA Ops:
  6.5 0.7 all-gather.2.cloned.1.call-update
  7.3 0.0 reduce-scatter.2.cloned.1.call-start
  7.4 0.1 broadcast_multiply_fusion
  7.4 0.1 pad_maximum_fusion.1
  7.6 0.0 copy-start.3
  7.6 2.6 %copy.25 = f32[2,64,128]{0,2,1:T(8,128)} copy(f32[2,64,128]{2,1,0:T(8,128)S(1)} %pad_maximum_fusion.1) | data formatting | bytes 131072 | tf_op jit(solution)/shard_map/concatenate | solution.py:31
  10.2 2.6 %copy.27 = f32[2,64,128]{0,2,1:T(8,128)} copy(f32[2,64,128]{2,1,0:T(8,128)S(1)} %copy-done.2) | data formatting | bytes 131072 | tf_op args[1]
  12.8 0.8 gather_fusion
  13.6 0.7 fusion.63
  14.4 0.1 slice_bitcast_fusion.1
  14.5 46.8 %all-gather.2.cloned.1.call-done = f32[64,64,128]{2,1,0:T(8,128)} async-done(((f32[8,64,128]{2,1,0:T(8,128)}), f32[64,64,128]{2,1,0:T(8,128)}) %all-gather.2.cloned.1.call-update) | async-done | bytes 2097168 | tf_op jit(solution)/shard_map/all_gather | solution.py:81
  61.3 3.8 %copy.26 = f32[64,64,128]{0,2,1:T(8,128)} copy(f32[64,64,128]{2,1,0:T(8,128)} %all-gather.2.cloned.1.call-done) | data formatting | bytes 4194304 | tf_op jit(solution)/shard_map/all_gather | solution.py:81
  65.1 22.3 %subtract_subtract_fusion = f32[2,64,64,128]{1,0,3,2:T(2,128)} fusion(f32[2,64,128]{0,2,1:T(8,128)} %copy.27, f32[64,64,128]{0,2,1:T(8,128)} %copy.26, f32[2,64,128]{0,2,1:T(8,128)} %copy.25), kind=kLoop, calls=%fused_computation.30 | loop fusion | flops 2097152 | bytes 6422528 | tf_op jit(solution)/shard_map/sub | solution.py:32
  87.4 7.8 %fusion.64 = (f32[2,64,64,64]{1,0,3,2:T(2,128)}, f32[2,64,64,64]{1,0,3,2:T(2,128)}) fusion(f32[2,64,64,128]{1,0,3,2:T(2,128)} %subtract_subtract_fusion), kind=kLoop, calls=%fused_computation.96 | loop fusion | bytes 8388608 | tf_op jit(solution)/shard_map/slice | solution.py:37
  95.3 2.9 %gather_fusion.1 = f32[64,2,64]{2,1,0:T(2,128)S(1)} fusion(f32[2,64,64,64]{1,0,3,2:T(2,128)} %get-tuple-element.83, s32[64]{0:T(128)S(1)} %or_bitcast_fusion), kind=kCustom, calls=%fused_computation.1 | custom fusion | bytes 66048 | tf_op jit(solution)/shard_map/jit(diagonal)/gather | solution.py:37
  98.2 0.1 copy.28
  98.3 3.0 %gather_fusion.2 = f32[64,2,64]{2,1,0:T(2,128)S(1)} fusion(f32[2,64,64,64]{1,0,3,2:T(2,128)} %get-tuple-element.84, s32[64]{0:T(128)S(1)} %or_bitcast_fusion), kind=kCustom, calls=%fused_computation.2 | custom fusion | bytes 66048 | tf_op jit(solution)/shard_map/jit(diagonal)/gather | solution.py:38
  101.2 0.1 copy.29
  101.4 2.3 multiply_subtract_fusion
  103.7 3.1 %pad_maximum_fusion = f32[2,64,64,128]{3,2,1,0:T(8,128)} fusion(f32[2,64,64,64]{3,2,1,0:T(8,128)S(1)} %get-tuple-element.86, f32[2,64,64,64]{3,2,1,0:T(8,128)S(1)} %get-tuple-element.85), kind=kLoop, calls=%fused_computation.31 | loop fusion | flops 1048576 | bytes 8388608 | tf_op jit(solution)/shard_map/concatenate | solution.py:46
  106.8 87.1 %while.11 = (s32[]{:T(128)}, f32[2,64,64,128]{3,2,1,0:T(8,128)}, s32[]{:T(128)}, s32[2]{0:T(128)S(1)}, f32[64,128]{1,0:T(8,128)S(1)}, /*index=5*/f32[64,64,128]{...) while((s32[]{:T(128)}, f32[2,64,64,128]{3,2,1,0:T(8,128)}, ...), condition=%wide.region_2.3_spmd.clone, body=%wide.region_1.2_spmd.clone.sunk | while | flops 3234856960 | bytes 56787048 | solution.py:63
  107.6 2.2 copy.51
  109.8 1.4 slice_negate_fusion.4
  111.3 8.9 %bitcast_subtract_fusion.2 = f32[2,64,64,128]{3,2,1,0:T(8,128)S(1)} fusion(f32[64,128]{1,0:T(8,128)S(1)} %get-tuple-element.171, f32[2,64,128]{2,1,0:T(8,128)S(1)} %get-tuple-element.174, f32[64,64,128]{2,1,0:T(8,128)S(1)} %get-tuple-element.172, f32[2,64,128]{2,1,0:T(8,128)S(1)} %get-tuple-element.173, ...), kind=kOutput, calls=%fused_computation.18.clone.1 | convolution fusion | flops 1617952768 | bytes 14843904 | tf_op jit(solution)/shard_map/while/body/...ij,...jl->...il/dot_general | solution.py:21
  120.2 3.5 %slice_negate_fusion.5 = (f32[2,64,64,64]{3,2,1,0:T(8,128)S(1)}, f32[2,64,64,64]{3,2,1,0:T(8,128)}) fusion(f32[2,64,64,128]{3,2,1,0:T(8,128)S(1)} %bitcast_subtract_fusion.2), kind=kLoop, calls=%fused_computation.16.clone.1 | loop fusion | flops 524288 | bytes 8388608 | tf_op jit(solution)/shard_map/while/body/neg | solution.py:16
  123.7 11.9 %bitcast_select_fusion.2 = f32[2,64,64,128]{3,2,1,0:T(8,128)} fusion(f32[2,64,64,128]{3,2,1,0:T(8,128)S(1)} %copy.51, f32[2,64,64,64]{3,2,1,0:T(8,128)} %get-tuple-element.147, f32[2,64,64,64]{3,2,1,0:T(8,128)S(1)} %get-tuple-element.148, f32[2,64,64,128]{3,2,1,0:T(8,128)S(1)} %bitcast_subtract_fusion.2, pred[2]{0:T(512)(128)(4,1)S(1)} %broadcast_compare_fusion.2), kind=kOutput, calls=%fused_computation.17.clone.1 | convolution fusion | flops 1615855616 | bytes 16777218 | tf_op jit(solution)/shard_map/while/body/...ij,...jl->...il/dot_general | solution.py:21
  136.3 2.2 copy.51
  138.5 1.4 slice_negate_fusion.4
  139.9 8.9 %bitcast_subtract_fusion.2 = f32[2,64,64,128]{3,2,1,0:T(8,128)S(1)} fusion(f32[64,128]{1,0:T(8,128)S(1)} %get-tuple-element.171, f32[2,64,128]{2,1,0:T(8,128)S(1)} %get-tuple-element.174, f32[64,64,128]{2,1,0:T(8,128)S(1)} %get-tuple-element.172, f32[2,64,128]{2,1,0:T(8,128)S(1)} %get-tuple-element.173, ...), kind=kOutput, calls=%fused_computation.18.clone.1 | convolution fusion | flops 1617952768 | bytes 14843904 | tf_op jit(solution)/shard_map/while/body/...ij,...jl->...il/dot_general | solution.py:21
  148.9 3.5 %slice_negate_fusion.5 = (f32[2,64,64,64]{3,2,1,0:T(8,128)S(1)}, f32[2,64,64,64]{3,2,1,0:T(8,128)}) fusion(f32[2,64,64,128]{3,2,1,0:T(8,128)S(1)} %bitcast_subtract_fusion.2), kind=kLoop, calls=%fused_computation.16.clone.1 | loop fusion | flops 524288 | bytes 8388608 | tf_op jit(solution)/shard_map/while/body/neg | solution.py:16
  152.4 11.9 %bitcast_select_fusion.2 = f32[2,64,64,128]{3,2,1,0:T(8,128)} fusion(f32[2,64,64,128]{3,2,1,0:T(8,128)S(1)} %copy.51, f32[2,64,64,64]{3,2,1,0:T(8,128)} %get-tuple-element.147, f32[2,64,64,64]{3,2,1,0:T(8,128)S(1)} %get-tuple-element.148, f32[2,64,64,128]{3,2,1,0:T(8,128)S(1)} %bitcast_subtract_fusion.2, pred[2]{0:T(512)(128)(4,1)S(1)} %broadcast_compare_fusion.2), kind=kOutput, calls=%fused_computation.17.clone.1 | convolution fusion | flops 1615855616 | bytes 16777218 | tf_op jit(solution)/shard_map/while/body/...ij,...jl->...il/dot_general | solution.py:21
  165.0 2.2 copy.51
  167.2 1.4 slice_negate_fusion.4
  168.6 8.9 %bitcast_subtract_fusion.2 = f32[2,64,64,128]{3,2,1,0:T(8,128)S(1)} fusion(f32[64,128]{1,0:T(8,128)S(1)} %get-tuple-element.171, f32[2,64,128]{2,1,0:T(8,128)S(1)} %get-tuple-element.174, f32[64,64,128]{2,1,0:T(8,128)S(1)} %get-tuple-element.172, f32[2,64,128]{2,1,0:T(8,128)S(1)} %get-tuple-element.173, ...), kind=kOutput, calls=%fused_computation.18.clone.1 | convolution fusion | flops 1617952768 | bytes 14843904 | tf_op jit(solution)/shard_map/while/body/...ij,...jl->...il/dot_general | solution.py:21
  177.6 3.5 %slice_negate_fusion.5 = (f32[2,64,64,64]{3,2,1,0:T(8,128)S(1)}, f32[2,64,64,64]{3,2,1,0:T(8,128)}) fusion(f32[2,64,64,128]{3,2,1,0:T(8,128)S(1)} %bitcast_subtract_fusion.2), kind=kLoop, calls=%fused_computation.16.clone.1 | loop fusion | flops 524288 | bytes 8388608 | tf_op jit(solution)/shard_map/while/body/neg | solution.py:16
  181.1 11.9 %bitcast_select_fusion.2 = f32[2,64,64,128]{3,2,1,0:T(8,128)} fusion(f32[2,64,64,128]{3,2,1,0:T(8,128)S(1)} %copy.51, f32[2,64,64,64]{3,2,1,0:T(8,128)} %get-tuple-element.147, f32[2,64,64,64]{3,2,1,0:T(8,128)S(1)} %get-tuple-element.148, f32[2,64,64,128]{3,2,1,0:T(8,128)S(1)} %bitcast_subtract_fusion.2, pred[2]{0:T(512)(128)(4,1)S(1)} %broadcast_compare_fusion.2), kind=kOutput, calls=%fused_computation.17.clone.1 | convolution fusion | flops 1615855616 | bytes 16777218 | tf_op jit(solution)/shard_map/while/body/...ij,...jl->...il/dot_general | solution.py:21
  193.9 9.2 %dot_general.18 = f32[2,64,2,64,64]{3,2,1,4,0:T(2,128)} reshape(f32[2,64,128,64]{2,1,3,0:T(8,128)} %bitcast.62) | data formatting | bytes 8388608 | tf_op jit(solution)/shard_map/k,fkij->fij/dot_general | solution.py:88
  203.1 12.3 %fusion.27 = f32[1,2,64,2,64]{4,0,3,2,1:T(1,128)S(1)} fusion(f32[2,64,2,64,64]{3,2,1,4,0:T(2,128)} %dot_general.18, s32[64]{0:T(128)S(1)} %gather_fusion, s32[]{:T(128)S(6)} %mul.134), kind=kOutput, calls=%fused_computation.28 | convolution fusion | flops 12584384 | bytes 4260100 | tf_op jit(solution)/shard_map/k,fkij->fij/dot_general | solution.py:88
  215.3 0.1 reshape.121
  215.4 0.6 copy.32
  216.1 0.0 reduce-scatter.2.cloned.1.call-update
  216.1 16.9 %reduce-scatter.2.cloned.1.call-done = f32[2,2,8,1,128]{4,2,1,0,3:T(8,128)} async-done(((f32[2,2,8,4,128]{4,2,1,0,3:T(8,128)}), f32[2,2,8,1,128]{4,2,1,0,3:T(8,128)}) %reduce-scatter.2.cloned.1.call-update) | async-done | bytes 16400 | tf_op jit(solution)/shard_map/reduce_scatter | solution.py:93
  233.0 1.3 copy.33
  234.4 5.5 %all-to-all-start = ((f32[2,2,8,1,128]{4,3,1,0,2:T(1,128)}), f32[2,2,8,1,128]{4,3,1,0,2:T(1,128)S(1)}, u32[]{:S(2)}, u32[]{:S(2)}) async-start(f32[2,2,8,1,128]{4,3,1,0,2:T(1,128)} %copy.33), calls=%async_computation.1 | async-start | bytes 32768 | tf_op jit(solution)/shard_map/all_to_all | solution.py:94
  239.9 0.6 convert_reduce_fusion
  240.5 6.0 %all-to-all-done = f32[2,2,8,1,128]{4,3,1,0,2:T(1,128)S(1)} async-done(((f32[2,2,8,1,128]{4,3,1,0,2:T(1,128)}), f32[2,2,8,1,128]{4,3,1,0,2:T(1,128)S(1)}, u32[]{:S(2)}, u32[]{:S(2)}) %all-to-all-start) | async-done | bytes 16416 | tf_op jit(solution)/shard_map/all_to_all | solution.py:94
  246.5 0.7 broadcast_divide_fusion
  247.1 0.6 copy.34
  (24 shorter events, 0.1 us)
Async XLA Ops:
  6.5 3.6 %copy-start.2 = (f32[2,64,128]{2,1,0:T(8,128)S(1)}, f32[2,64,128]{2,1,0:T(8,128)}, u32[]{:S(2)}) copy-start(f32[2,64,128]{2,1,0:T(8,128)} %param.8) | copy-start | bytes 196612
  6.5 54.8 %all-gather.2.cloned.1.call-start = ((), (), s32[]{:S(2)}) async-start(), calls=%async_computation.2 | async-start | bytes 2359296 | tf_op jit(solution)/shard_map/all_gather | solution.py:81
  7.3 225.8 %reduce-scatter.2.cloned.1.call-start = ((), (), s32[]{:S(2)}) async-start(), calls=%async_computation.3 | async-start | bytes 81920 | tf_op jit(solution)/shard_map/reduce_scatter | solution.py:93
  7.5 5.3 %copy-start = (s32[256]{0:T(256)S(1)}, s32[256]{0:T(256)}, u32[]{:S(2)}) copy-start(s32[256]{0:T(256)} %param.10) | copy-start | bytes 3076
  7.5 6.1 %copy-start.4 = (s32[16]{0:T(128)S(1)}, s32[16]{0:T(128)}, u32[]{:S(2)}) copy-start(s32[16]{0:T(128)} %param.11) | copy-start | bytes 196
  7.6 6.8 %copy-start.3 = (f32[2,64,128]{2,1,0:T(8,128)S(1)}, f32[2,64,128]{2,1,0:T(8,128)}, u32[]{:S(2)}) copy-start(f32[2,64,128]{2,1,0:T(8,128)} %param.9) | copy-start | bytes 196612
  103.7 3.1 %copy-start.1 = (f32[64,64,128]{2,1,0:T(8,128)S(1)}, f32[64,64,128]{2,1,0:T(8,128)}, u32[]{:S(2)}) copy-start(f32[64,64,128]{2,1,0:T(8,128)} %all-gather.2.cloned.1.call-done) | copy-start | bytes 6291460
  234.4 12.1 %all-to-all-start = ((f32[2,2,8,1,128]{4,3,1,0,2:T(1,128)}), f32[2,2,8,1,128]{4,3,1,0,2:T(1,128)S(1)}, u32[]{:S(2)}, u32[]{:S(2)}) async-start(f32[2,2,8,1,128]{4,3,1,0,2:T(1,128)} %copy.33), calls=%async_computation.1 | async-start | bytes 32768 | tf_op jit(solution)/shard_map/all_to_all | solution.py:94
Sparse Core Ops, SparseCore 0:
  9.5 51.7 all-gather.1
  216.2 16.7 reduce-scatter.1
where the time goes:
time: 255 us
  matrix products  74.9 us (29%)
  waiting for transfers between devices  70.5 us (28%)
  other arithmetic  44.8 us (18%)
  local copies, waits for them, and re-layouts  42.3 us (17%)
  between operations  13.6 us (5%)
  starting transfers between devices  5.57 us (2%)
  loops' own time  3.03 us (1%)
    dot_general x6, matrix products, complex_product(): jnp.einsum('...ij,...jl->...il', left_side, blockify(right_side), precisi...  62.6 us
    all_gather x1, waiting for transfers between devices, per_device(): h_piece = lax.all_gather(hamiltonian, 'freq', axis=0, tiled=True)  46.8 us
    sub x1, other arithmetic, build_matrix(): return diagonal_shift[:, None] - kpoint_rows[None] - sigma_rows[:, None]  22.3 us
    reduce_scatter x1, waiting for transfers between devices, per_device(): lax.psum_scatter(partial_term, 'kgrp', scatter_dimension=3, tiled=True)  16.9 us
    neg x6, other arithmetic, blockify(): lower_row = jnp.concatenate([-imag_part, real_part], -1)  14.8 us
    dot_general x1, matrix products, per_device(): jnp.einsum('k,fkij->fij', factors, inverses, precision=lax.Precision.HIGH...  12.3 us
    dot_general x2, local copies, waits for them, and re-layouts, per_device(): jnp.einsum('k,fkij->fij', factors, inverses, precision=lax.Precision.HIGH...  9.2 us
    slice x1, local copies, waits for them, and re-layouts, start_guess(): diag_real = jnp.diagonal(matrix[..., :orbitals], axis1=-2, axis2=-1)  7.83 us
  transfers between devices with their start and end apart: 3, of which 3 were waited for; matrix products, arithmetic and copies ran while one was open for 3% of the time, Pallas kernels for 0%

commit v1 on v0

v1 whole, which is shorter than its diff:
```python
import functools
import math

import jax
import jax.numpy as jnp
from jax import lax
from jax.experimental import pallas as pl
from jax.experimental.pallas import tpu as pltpu
from jax.sharding import PartitionSpec as P

chem_potential = 0.2
MESH = pl.DeviceIdType.MESH
VMEM = pl.BlockSpec(memory_space=pltpu.VMEM)
SMEM = pl.BlockSpec(memory_space=pltpu.SMEM)


def split(value):
    high = value.astype(jnp.bfloat16).astype(jnp.float32)
    return high, value - high


def left_operand(value, half, left):
    high, low = split(value)
    turned_high, turned_low = split(pltpu.roll(value, half, 1))
    top = jnp.where(left, high, turned_low)
    bottom = jnp.where(left, turned_high, low)
    return jnp.concatenate([top, bottom], 0).astype(jnp.bfloat16)


def right_operand(value):
    high, low = split(value)
    row = jnp.concatenate([high, low], 1).astype(jnp.bfloat16)
    return jnp.concatenate([row, row], 0)


def fold(product, orbitals, sign):
    width = 2 * orbitals
    both = product[:, :width] + product[:, width:]
    return both[:orbitals] + sign * pltpu.roll(both[orbitals:], orbitals, 1)


def invert_kernel(
    counts, weights, h_ref, sigma_ref, guess_ref, out_ref, m_left, x_now, h_diag, last_left, last_right
):
    k_local, orbitals, width = h_ref.shape
    freq_total = sigma_ref.shape[0]
    shape = (orbitals, width)
    row = lax.broadcasted_iota(jnp.int32, shape, 0)
    lane = lax.broadcasted_iota(jnp.int32, shape, 1)
    left = lane < orbitals
    sign = jnp.where(left, -1.0, 1.0)
    eye_real = (lane == row).astype(jnp.float32)
    eye_imag = (lane == row + orbitals).astype(jnp.float32)
    device = lax.axis_index("freq") * lax.axis_size("kgrp") + lax.axis_index("kgrp")

    def add_weight(index, total):
        return total + weights[index]

    weight_total = lax.fori_loop(
        0, weights.shape[0], add_weight, jnp.int32(0), unroll=8
    ).astype(jnp.float32)
    factors = [
        jnp.full((1, width), weights[device * k_local + k].astype(jnp.float32)) / weight_total
        for k in range(k_local)
    ]

    def diagonal(value):
        real = jnp.sum(value * eye_real, axis=1, keepdims=True)
        imag = jnp.sum(value * eye_imag, axis=1, keepdims=True)
        return jnp.broadcast_to(real, shape), jnp.broadcast_to(imag, shape)

    for k in range(k_local):
        h_diag[0, k], h_diag[1, k] = diagonal(h_ref[k])

    def one_frequency(freq, carry):
        matsubara = (2 * freq + 1).astype(jnp.float32) * (math.pi / (2 * freq_total))
        base = (chem_potential * eye_real + matsubara * eye_imag) - sigma_ref[freq]
        base_real, base_imag = diagonal(base)
        guess = guess_ref[freq]
        turned = sign * pltpu.roll(guess, orbitals, 1)
        for k in range(k_local):
            matrix = base - h_ref[k]
            m_left[k] = left_operand(matrix, orbitals, left)
            real = base_real - h_diag[0, k]
            imag = base_imag - h_diag[1, k]
            inverse = 1.0 / (real * real + imag * imag)
            x_now[k] = (real * inverse) * guess - (imag * inverse) * turned

        def residual(k, current):
            product = jnp.dot(
                m_left[k], right_operand(current), preferred_element_type=jnp.float32
            )
            return eye_real - fold(product, orbitals, sign)

        def newton_step(sweep, inner):
            for k in range(k_local):
                current = x_now[k]
                missing = residual(k, current)
                product = jnp.dot(
                    left_operand(current, orbitals, left),
                    right_operand(missing),
                    preferred_element_type=jnp.float32,
                )
                x_now[k] = current + fold(product, orbitals, sign)
            return inner

        lax.fori_loop(0, counts[freq] - 1, newton_step, 0)
        total = jnp.zeros(shape, jnp.float32)
        for k in range(k_local):
            current = x_now[k]
            last_right[k * width : (k + 1) * width, :] = right_operand(residual(k, current))
            weighted = current * factors[k]
            last_left[:, k * width : (k + 1) * width] = left_operand(weighted, orbitals, left)
            total = total + weighted
        product = jnp.dot(last_left[...], last_right[...], preferred_element_type=jnp.float32)
        total = total + fold(product, orbitals, sign)
        out_ref[pl.ds(freq, orbitals, stride=freq_total), :] = total
        return carry

    lax.fori_loop(0, freq_total, one_frequency, 0)


def invert(counts, weights, hamiltonian, sigma, guess):
    k_local, orbitals, width = hamiltonian.shape
    freq_total = sigma.shape[0]
    return pl.pallas_call(
        invert_kernel,
        out_shape=jax.ShapeDtypeStruct((orbitals * freq_total, width), jnp.float32),
        in_specs=[SMEM, SMEM, VMEM, VMEM, VMEM],
        out_specs=VMEM,
        scratch_shapes=[
            pltpu.VMEM((k_local, width, width), jnp.bfloat16),
            pltpu.VMEM((k_local, orbitals, width), jnp.float32),
            pltpu.VMEM((2, k_local, orbitals, width), jnp.float32),
            pltpu.VMEM((width, k_local * width), jnp.bfloat16),
            pltpu.VMEM((k_local * width, 2 * width), jnp.bfloat16),
        ],
        name="invert",
    )(counts, weights, hamiltonian, sigma, guess)


def gather_kernel(sigma_ref, guess_ref, out_sigma, out_guess, local_sem, send, recv, pass_send, pass_recv):
    per_freq = sigma_ref.shape[0]
    freq_devs = lax.axis_size("freq")
    me = lax.axis_index("freq")
    group = lax.axis_index("kgrp")
    parity = lax.rem(group, 2)
    mate = group + 1 - 2 * parity
    barrier = pltpu.get_barrier_semaphore()
    for shift in range(1, freq_devs):
        pl.semaphore_signal(
            barrier, inc=1, device_id=(lax.rem(me + shift, freq_devs), group), device_id_type=MESH
        )
    pl.semaphore_signal(barrier, inc=1, device_id=(me, mate), device_id_type=MESH)
    own = pl.ds(me * per_freq, per_freq)
    keeps = [
        pltpu.make_async_copy(sigma_ref, out_sigma.at[own], local_sem.at[0]),
        pltpu.make_async_copy(guess_ref, out_guess.at[own], local_sem.at[1]),
    ]
    for keep in keeps:
        keep.start()
    pl.semaphore_wait(barrier, freq_devs)

    def exchange(source, target):
        copies = []
        for shift in range(1, freq_devs):
            copies.append(
                pltpu.make_async_remote_copy(
                    src_ref=source,
                    dst_ref=target.at[own],
                    send_sem=send.at[shift],
                    recv_sem=recv.at[shift],
                    device_id=(lax.rem(me + shift, freq_devs), group),
                    device_id_type=MESH,
                )
            )
        for copy in copies:
            copy.start()
        passes = []
        for shift in range(1, freq_devs):
            copies[shift - 1].wait_recv()
            origin = lax.rem(me - shift + freq_devs, freq_devs)
            landed = target.at[pl.ds(origin * per_freq, per_freq)]
            forward = pltpu.make_async_remote_copy(
                src_ref=landed,
                dst_ref=landed,
                send_sem=pass_send.at[shift],
                recv_sem=pass_recv.at[shift],
                device_id=(me, mate),
                device_id_type=MESH,
            )
            forward.start()
            passes.append(forward)
        for forward in passes:
            forward.wait()
        for copy in copies:
            copy.wait_send()

    @pl.when(parity == 0)
    def _():
        exchange(sigma_ref, out_sigma)

    @pl.when(parity == 1)
    def _():
        exchange(guess_ref, out_guess)

    for keep in keeps:
        keep.wait()


def gather(self_energy, guess_factor, freq_devs):
    per_freq, orbitals, width = self_energy.shape
    full = jax.ShapeDtypeStruct((per_freq * freq_devs, orbitals, width), jnp.float32)
    return pl.pallas_call(
        gather_kernel,
        out_shape=(full, full),
        in_specs=[VMEM, VMEM],
        out_specs=(VMEM, VMEM),
        scratch_shapes=[
            pltpu.SemaphoreType.DMA((2,)),
            pltpu.SemaphoreType.DMA((freq_devs,)),
            pltpu.SemaphoreType.DMA((freq_devs,)),
            pltpu.SemaphoreType.DMA((freq_devs,)),
            pltpu.SemaphoreType.DMA((freq_devs,)),
        ],
        compiler_params=pltpu.CompilerParams(collective_id=0, has_side_effects=True),
        name="gather",
    )(self_energy, guess_factor)


def scatter_kernel(part_ref, out_ref, mate_half, summed, landed, mate_sems, send, recv):
    freq_devs, pairs, _, rows, width = part_ref.shape
    me = lax.axis_index("freq")
    group = lax.axis_index("kgrp")
    half = group // 2
    parity = lax.rem(group, 2)
    mate = group + 1 - 2 * parity
    others = [(a, b) for a in range(freq_devs) for b in range(pairs) if a + b > 0]
    barrier = pltpu.get_barrier_semaphore()

    def place(step, back=False):
        a, b = step
        if back:
            a, b = freq_devs - a, pairs - b
        return lax.rem(me + a, freq_devs), lax.rem(half + b, pairs)

    for step in others:
        freq_to, half_to = place(step)
        pl.semaphore_signal(
            barrier, inc=1, device_id=(freq_to, 2 * half_to + parity), device_id_type=MESH
        )
    pl.semaphore_signal(barrier, inc=1, device_id=(me, mate), device_id_type=MESH)
    pl.semaphore_wait(barrier, len(others) + 1)
    swaps = []
    for freq_to in range(freq_devs):
        swap = pltpu.make_async_remote_copy(
            src_ref=part_ref.at[freq_to, :, 1 - parity],
            dst_ref=mate_half.at[freq_to],
            send_sem=mate_sems.at[0, freq_to],
            recv_sem=mate_sems.at[1, freq_to],
            device_id=(me, mate),
            device_id_type=MESH,
        )
        swap.start()
        swaps.append(swap)
    for freq_to in range(freq_devs):
        swaps[freq_to].wait_recv()
        for half_to in range(pairs):
            summed[freq_to, half_to] = (
                part_ref[freq_to, half_to, parity] + mate_half[freq_to, half_to]
            )
    copies = []
    for index, step in enumerate(others):
        freq_to, half_to = place(step)
        copy = pltpu.make_async_remote_copy(
            src_ref=summed.at[freq_to, half_to],
            dst_ref=landed.at[index],
            send_sem=send.at[index],
            recv_sem=recv.at[index],
            device_id=(freq_to, 2 * half_to + parity),
            device_id_type=MESH,
        )
        copy.start()
        copies.append(copy)
    total = summed[me, half]
    for index, copy in enumerate(copies):
        copy.wait_recv()
        total = total + landed[index]
    out_ref[...] = total
    for copy in copies:
        copy.wait_send()
    for swap in swaps:
        swap.wait_send()


def scatter(partial, freq_devs, group_devs):
    rows, width = partial.shape
    pairs = group_devs // 2
    own_rows = rows // (freq_devs * group_devs)
    peers = freq_devs * pairs - 1
    block = (own_rows, width)
    return pl.pallas_call(
        scatter_kernel,
        out_shape=jax.ShapeDtypeStruct(block, jnp.float32),
        in_specs=[VMEM],
        out_specs=VMEM,
        scratch_shapes=[
            pltpu.VMEM((freq_devs, pairs) + block, jnp.float32),
            pltpu.VMEM((freq_devs, pairs) + block, jnp.float32),
            pltpu.VMEM((peers,) + block, jnp.float32),
            pltpu.SemaphoreType.DMA((2, freq_devs)),
            pltpu.SemaphoreType.DMA((peers,)),
            pltpu.SemaphoreType.DMA((peers,)),
        ],
        compiler_params=pltpu.CompilerParams(collective_id=1, has_side_effects=True),
        name="scatter",
    )(partial.reshape(freq_devs, pairs, 2, own_rows, width))


def per_device(hamiltonian, self_energy, guess_factor, weights, counts):
    orbitals = hamiltonian.shape[1]
    per_freq = self_energy.shape[0]
    freq_devs = lax.axis_size("freq")
    group_devs = lax.axis_size("kgrp")
    freq_total = per_freq * freq_devs
    pair_block = orbitals * orbitals // (freq_devs * group_devs)
    direct = pair_block % orbitals == 0 and group_devs % 2 == 0
    if direct:
        sigma, guess = gather(self_energy, guess_factor, freq_devs)
    else:
        sigma = lax.all_gather(self_energy, "freq", axis=0, tiled=True)
        guess = lax.all_gather(guess_factor, "freq", axis=0, tiled=True)
    partial = invert(counts, weights, hamiltonian, sigma, guess)
    if direct:
        own = scatter(partial, freq_devs, group_devs)
        own = own.reshape(pair_block // orbitals, freq_total, 2, orbitals)
        result = own.transpose(0, 3, 2, 1)
    else:
        terms = partial.reshape(orbitals, freq_total, 2, orbitals).transpose(0, 3, 2, 1)
        terms = terms.reshape(orbitals * orbitals, 2 * freq_total)
        result = lax.psum_scatter(terms, ("freq", "kgrp"), scatter_dimension=0, tiled=True)
    return result.reshape(pair_block, 2 * freq_total)


def solution(mesh):
    return jax.shard_map(
        per_device,
        mesh=mesh,
        in_specs=(
            P(("freq", "kgrp"), None, None),
            P("freq", None, None),
            P("freq", None, None),
            P(),
            P(),
        ),
        out_specs=P(("freq", "kgrp"), None),
        check_vma=False,
    )
```

time: 255 us -> 59.2 us (0.23)
  matrix products: 74.9 us -> 0 us
  waiting for transfers between devices: 70.5 us -> 0 us
  Pallas kernels: 0 us -> 58.1 us
  other arithmetic: 44.8 us -> 0 us
  local copies, waits for them, and re-layouts: 42.3 us -> 1.52 us
  between operations: 13.6 us -> 0.03 us
  starting transfers between devices: 5.57 us -> 0 us
  loops' own time: 3.03 us -> 0 us
    dot_general x7 -> x0, matrix products: 74.9 us -> none  [the longest x6 62.6 us: complex_product(): jnp.einsum('...ij,...jl->...il', left_side, blockify(right_side), precisi...]
    pallas_call x0 -> x3, Pallas kernels: none -> 58.1 us  [the longest x1 23.6 us: invert(): pl.pallas_call(invert_kernel, out_shape=jax.ShapeDtypeStruct((orbitals *...]
    all_gather x1 -> x0, waiting for transfers between devices: 46.8 us -> none  [per_device(): h_piece = lax.all_gather(hamiltonian, 'freq', axis=0, tiled=True)]
    sub x2 -> x0, other arithmetic: 24.6 us -> none  [the longest x1 22.3 us: build_matrix(): return diagonal_shift[:, None] - kpoint_rows[None] - sigma_rows[:, None]]
    reduce_scatter x1 -> x0, waiting for transfers between devices: 16.9 us -> none  [per_device(): lax.psum_scatter(partial_term, 'kgrp', scatter_dimension=3, tiled=True)]
    neg x6 -> x0, other arithmetic: 14.8 us -> none  [blockify(): lower_row = jnp.concatenate([-imag_part, real_part], -1)]
    dot_general x2 -> x0, local copies, waits for them, and re-layouts: 9.2 us -> none  [per_device(): jnp.einsum('k,fkij->fij', factors, inverses, precision=lax.Precision.HIGH...]
    slice x1 -> x0, local copies, waits for them, and re-layouts: 7.83 us -> none  [start_guess(): diag_real = jnp.diagonal(matrix[..., :orbitals], axis1=-2, axis2=-1)]
  transfers between devices with their start and end apart: 3 -> 0, of which waited for: 3 -> 0; matrix products, arithmetic and copies ran while one was open for 3% -> 0% of each run, Pallas kernels for 0% -> 0%
where the time goes in v1:
time: 59.2 us; the launch traced here: 59.7 us
  Pallas kernels  58.1 us (98%)
  local copies, waits for them, and re-layouts  1.52 us (3%)
    pallas_call x1, Pallas kernels, invert(): pl.pallas_call(invert_kernel, out_shape=jax.ShapeDtypeStruct((orbitals *...  23.6 us
    pallas_call x1, Pallas kernels, gather(): pl.pallas_call(gather_kernel, out_shape=(full, full), in_specs=[VMEM, VME...  18 us
    pallas_call x1, Pallas kernels, scatter(): pl.pallas_call(scatter_kernel, out_shape=jax.ShapeDtypeStruct(block, jnp....  16.6 us

profile of v1, /device:TPU:0, one launch (start us, length us, event | category | flops | bytes accessed | tf_op | source)
XLA Modules:
  0.0 59.7 jit_solution(8719457059021013257)
XLA Ops:
  0.0 18.0 %gather.1 = (f32[16,64,128]{2,1,0:T(8,128)}, f32[16,64,128]{2,1,0:T(8,128)}) custom-call(f32[2,64,128]{2,1,0:T(8,128)} %sigma_ref.1, f32[2,64,128]{2,1,0:T(8,128)} %guess_ref.1), custom_call_target="tpu_custom_call" | custom-call | tf_op jit(solution)/shard_map/gather/pallas_call | solution.py:214
  18.0 23.6 %invert.1 = f32[1024,128]{1,0:T(8,128)} custom-call(s32[16]{0:T(128)} %counts.1, s32[256]{0:T(256)} %weights.1, f32[8,64,128]{2,1,0:T(8,128)} %h_ref.1, f32[16,64,128]{2,1,0:T(8,128)} %get-tuple-element.7.sigma_ref, f32[16,64,128]{2,1,0:T(8,128)} %get-tuple-element.8.guess_ref), custom_call_target="tpu_custom_call" | custom-call | tf_op jit(solution)/shard_map/invert/pallas_call | solution.py:126
  41.5 16.6 %scatter.1 = f32[32,128]{1,0:T(8,128)} custom-call(f32[8,2,2,32,128]{4,3,2,1,0:T(8,128)} %bitcast.4), custom_call_target="tpu_custom_call" | custom-call | tf_op jit(solution)/shard_map/scatter/pallas_call | solution.py:302
  58.1 0.8 %reshape.10 = f32[2,16,2,64]{3,2,1,0:T(2,128)S(1)} reshape(f32[32,128]{1,0:T(8,128)} %scatter.1) | data formatting | bytes 32768 | tf_op jit(solution)/shard_map/reshape | solution.py:336
  59.0 0.7 %reshape.11 = f32[128,32]{0,1:T(8,128)} reshape(f32[2,64,2,16]{1,0,3,2:T(2,128)S(1)} %copy.6) | data formatting | bytes 32768 | tf_op jit(solution)/shard_map/reshape | solution.py:342
  (1 shorter events, 0.0 us)

commit v2 on v1

v2 whole, which is shorter than its diff:
```python
import functools
import math

import jax
import jax.numpy as jnp
from jax import lax
from jax.experimental import pallas as pl
from jax.experimental.pallas import tpu as pltpu
from jax.sharding import PartitionSpec as P

chem_potential = 0.2
MESH = pl.DeviceIdType.MESH
VMEM = pl.BlockSpec(memory_space=pltpu.VMEM)
SMEM = pl.BlockSpec(memory_space=pltpu.SMEM)


def split(value):
    high = value.astype(jnp.bfloat16).astype(jnp.float32)
    return high, value - high


def left_operand(value, half, left):
    high, low = split(value)
    turned_high, turned_low = split(pltpu.roll(value, half, 1))
    top = jnp.where(left, high, turned_low)
    bottom = jnp.where(left, turned_high, low)
    return jnp.concatenate([top, bottom], 0).astype(jnp.bfloat16)


def right_operand(value):
    high, low = split(value)
    row = jnp.concatenate([high, low], 1).astype(jnp.bfloat16)
    return jnp.concatenate([row, row], 0)


def fold(product, orbitals, sign):
    width = 2 * orbitals
    both = product[:, :width] + product[:, width:]
    return both[:orbitals] + sign * pltpu.roll(both[orbitals:], orbitals, 1)


def masks(shape):
    orbitals = shape[0]
    row = lax.broadcasted_iota(jnp.int32, shape, 0)
    lane = lax.broadcasted_iota(jnp.int32, shape, 1)
    left = lane < orbitals
    sign = jnp.where(left, -1.0, 1.0)
    eye_real = (lane == row).astype(jnp.float32)
    eye_imag = (lane == row + orbitals).astype(jnp.float32)
    return left, sign, eye_real, eye_imag


def shifted(freq, freq_total, eye_real, eye_imag, sigma):
    matsubara = (2 * freq + 1).astype(jnp.float32) * (math.pi / (2 * freq_total))
    return (chem_potential * eye_real + matsubara * eye_imag) - sigma


def steps_kernel(counts, weights, h_ref, sigma_ref, guess_ref, x_ref, factor_ref, m_left, h_diag):
    k_local, orbitals, width = h_ref.shape
    freq_total = sigma_ref.shape[0]
    shape = (orbitals, width)
    left, sign, eye_real, eye_imag = masks(shape)
    device = lax.axis_index("freq") * lax.axis_size("kgrp") + lax.axis_index("kgrp")

    def add_weight(index, total):
        return total + weights[index]

    weight_total = lax.fori_loop(
        0, weights.shape[0], add_weight, jnp.int32(0), unroll=8
    ).astype(jnp.float32)
    for k in range(k_local):
        weight = weights[device * k_local + k].astype(jnp.float32)
        factor_ref[k : k + 1, :] = jnp.full((1, width), weight) / weight_total

    def diagonal(value):
        real = jnp.sum(value * eye_real, axis=1, keepdims=True)
        imag = jnp.sum(value * eye_imag, axis=1, keepdims=True)
        return jnp.broadcast_to(real, shape), jnp.broadcast_to(imag, shape)

    for k in range(k_local):
        h_diag[0, k], h_diag[1, k] = diagonal(h_ref[k])

    def one_frequency(freq, carry):
        base = shifted(freq, freq_total, eye_real, eye_imag, sigma_ref[freq])
        base_real, base_imag = diagonal(base)
        guess = guess_ref[freq]
        turned = sign * pltpu.roll(guess, orbitals, 1)
        for k in range(k_local):
            real = base_real - h_diag[0, k]
            imag = base_imag - h_diag[1, k]
            inverse = 1.0 / (real * real + imag * imag)
            x_ref[freq, k] = (real * inverse) * guess - (imag * inverse) * turned

        @pl.when(counts[freq] > 1)
        def _():
            for k in range(k_local):
                m_left[k] = left_operand(base - h_ref[k], orbitals, left)

            def newton_step(sweep, inner):
                for k in range(k_local):
                    current = x_ref[freq, k]
                    product = jnp.dot(
                        m_left[k], right_operand(current), preferred_element_type=jnp.float32
                    )
                    missing = eye_real - fold(product, orbitals, sign)
                    product = jnp.dot(
                        left_operand(current, orbitals, left),
                        right_operand(missing),
                        preferred_element_type=jnp.float32,
                    )
                    x_ref[freq, k] = current + fold(product, orbitals, sign)
                return inner

            lax.fori_loop(0, counts[freq] - 1, newton_step, 0)

        return carry

    lax.fori_loop(0, freq_total, one_frequency, 0)


def early_steps(counts, weights, hamiltonian, sigma, guess):
    k_local, orbitals, width = hamiltonian.shape
    freq_total = sigma.shape[0]
    return pl.pallas_call(
        steps_kernel,
        out_shape=(
            jax.ShapeDtypeStruct((freq_total, k_local, orbitals, width), jnp.float32),
            jax.ShapeDtypeStruct((k_local, width), jnp.float32),
        ),
        in_specs=[SMEM, SMEM, VMEM, VMEM, VMEM],
        out_specs=(VMEM, VMEM),
        scratch_shapes=[
            pltpu.VMEM((k_local, width, width), jnp.bfloat16),
            pltpu.VMEM((2, k_local, orbitals, width), jnp.float32),
        ],
        name="early_steps",
    )(counts, weights, hamiltonian, sigma, guess)


def last_step(freq, freq_total, factor_ref, h_ref, sigma_ref, x_ref, last_left, last_right):
    k_local, orbitals, width = h_ref.shape
    left, sign, eye_real, eye_imag = masks((orbitals, width))
    base = shifted(freq, freq_total, eye_real, eye_imag, sigma_ref[freq])
    total = jnp.zeros((orbitals, width), jnp.float32)
    for k in range(k_local):
        current = x_ref[freq, k]
        product = jnp.dot(
            left_operand(base - h_ref[k], orbitals, left),
            right_operand(current),
            preferred_element_type=jnp.float32,
        )
        missing = eye_real - fold(product, orbitals, sign)
        last_right[k * width : (k + 1) * width, :] = right_operand(missing)
        weighted = current * factor_ref[k : k + 1, :]
        last_left[:, k * width : (k + 1) * width] = left_operand(weighted, orbitals, left)
        total = total + weighted
    product = jnp.dot(last_left[...], last_right[...], preferred_element_type=jnp.float32)
    return total + fold(product, orbitals, sign)


def last_scratch(k_local, width):
    return [
        pltpu.VMEM((width, k_local * width), jnp.bfloat16),
        pltpu.VMEM((k_local * width, 2 * width), jnp.bfloat16),
    ]


def sum_kernel(factor_ref, h_ref, sigma_ref, x_ref, out_ref, last_left, last_right):
    freq_total = sigma_ref.shape[0]

    def one_frequency(freq, carry):
        out_ref[freq] = last_step(
            freq, freq_total, factor_ref, h_ref, sigma_ref, x_ref, last_left, last_right
        )
        return carry

    lax.fori_loop(0, freq_total, one_frequency, 0)


def local_sum(factors, hamiltonian, sigma, current):
    k_local, orbitals, width = hamiltonian.shape
    return pl.pallas_call(
        sum_kernel,
        out_shape=jax.ShapeDtypeStruct(sigma.shape, jnp.float32),
        in_specs=[VMEM] * 4,
        out_specs=VMEM,
        scratch_shapes=last_scratch(k_local, width),
        name="local_sum",
    )(factors, hamiltonian, sigma, current)


def gather_kernel(
    sigma_ref, guess_ref, out_sigma, out_guess, local_sem, send, recv, side_send, side_recv, pass_send, pass_recv
):
    per_freq = sigma_ref.shape[0]
    freq_devs = lax.axis_size("freq")
    column = freq_devs // 2
    me = lax.axis_index("freq")
    group = lax.axis_index("kgrp")
    parity = lax.rem(group, 2)
    mate = group + 1 - 2 * parity
    beside = me + 1 - 2 * lax.rem(me, 2)
    barrier = pltpu.get_barrier_semaphore()
    for shift in range(1, column):
        pl.semaphore_signal(
            barrier, inc=1, device_id=(lax.rem(me + 2 * shift, freq_devs), group), device_id_type=MESH
        )
    pl.semaphore_signal(barrier, inc=1, device_id=(beside, group), device_id_type=MESH)
    pl.semaphore_signal(barrier, inc=1, device_id=(me, mate), device_id_type=MESH)
    own = pl.ds(me * per_freq, per_freq)
    keeps = [
        pltpu.make_async_copy(sigma_ref, out_sigma.at[own], local_sem.at[0]),
        pltpu.make_async_copy(guess_ref, out_guess.at[own], local_sem.at[1]),
    ]
    for keep in keeps:
        keep.start()
    pl.semaphore_wait(barrier, column + 1)

    def exchange(source, target):
        def piece(origin):
            return target.at[pl.ds(origin * per_freq, per_freq)]

        def remote(src, dst, send_sem, recv_sem, freq_to, group_to):
            copy = pltpu.make_async_remote_copy(
                src_ref=src,
                dst_ref=dst,
                send_sem=send_sem,
                recv_sem=recv_sem,
                device_id=(freq_to, group_to),
                device_id_type=MESH,
            )
            copy.start()
            return copy

        along = {}
        for shift in range(1, column):
            freq_to = lax.rem(me + 2 * shift, freq_devs)
            along[shift] = remote(
                source, piece(me), send.at[shift], recv.at[shift], freq_to, group
            )
        across = [remote(source, piece(me), side_send.at[0], side_recv.at[0], beside, group)]
        passes = []

        def hand(origin):
            slot = len(passes)
            landed = piece(origin)
            passes.append(
                remote(landed, landed, pass_send.at[slot], pass_recv.at[slot], me, mate)
            )

        for shift in range(1, column):
            along[shift].wait_recv()
            origin = lax.rem(me - 2 * shift + freq_devs, freq_devs)
            landed = piece(origin)
            across.append(
                remote(landed, landed, side_send.at[shift], side_recv.at[shift], beside, group)
            )
            hand(origin)
        for shift in range(column):
            across[shift].wait_recv()
            hand(lax.rem(beside - 2 * shift + freq_devs, freq_devs))
        for copy in passes:
            copy.wait()
        for copy in list(along.values()) + across:
            copy.wait_send()

    @pl.when(parity == 0)
    def _():
        exchange(sigma_ref, out_sigma)

    @pl.when(parity == 1)
    def _():
        exchange(guess_ref, out_guess)

    for keep in keeps:
        keep.wait()


def gather(self_energy, guess_factor, freq_devs):
    per_freq, orbitals, width = self_energy.shape
    full = jax.ShapeDtypeStruct((per_freq * freq_devs, orbitals, width), jnp.float32)
    sems = pltpu.SemaphoreType.DMA((freq_devs,))
    return pl.pallas_call(
        gather_kernel,
        out_shape=(full, full),
        in_specs=[VMEM, VMEM],
        out_specs=(VMEM, VMEM),
        scratch_shapes=[pltpu.SemaphoreType.DMA((2,))] + [sems] * 6,
        compiler_params=pltpu.CompilerParams(collective_id=0, has_side_effects=True),
        name="gather",
    )(self_energy, guess_factor)


def scatter_kernel(
    factor_ref,
    h_ref,
    sigma_ref,
    x_ref,
    out_ref,
    last_left,
    last_right,
    part,
    mate_half,
    summed,
    landed,
    mate_send,
    mate_recv,
    send,
    recv,
):
    chunks, freq_devs, pairs, _, rows, width = part.shape
    orbitals = h_ref.shape[1]
    freq_total = sigma_ref.shape[0]
    per_chunk = freq_total // chunks
    me = lax.axis_index("freq")
    group = lax.axis_index("kgrp")
    half = group // 2
    parity = lax.rem(group, 2)
    mate = group + 1 - 2 * parity
    others = [(a, b) for a in range(freq_devs) for b in range(pairs) if a + b > 0]
    barrier = pltpu.get_barrier_semaphore()
    flat = part.reshape(chunks, orbitals * per_chunk, width)

    def place(step):
        return lax.rem(me + step[0], freq_devs), lax.rem(half + step[1], pairs)

    for step in others:
        freq_to, half_to = place(step)
        pl.semaphore_signal(
            barrier, inc=1, device_id=(freq_to, 2 * half_to + parity), device_id_type=MESH
        )
    pl.semaphore_signal(barrier, inc=1, device_id=(me, mate), device_id_type=MESH)

    def swap(chunk):
        return pltpu.make_async_remote_copy(
            src_ref=part.at[chunk, :, :, 1 - parity],
            dst_ref=mate_half.at[chunk],
            send_sem=mate_send.at[chunk],
            recv_sem=mate_recv.at[chunk],
            device_id=(me, mate),
            device_id_type=MESH,
        )

    def spread(chunk, index):
        freq_to, half_to = place(others[index])
        return pltpu.make_async_remote_copy(
            src_ref=summed.at[chunk, freq_to, half_to],
            dst_ref=landed.at[chunk, index],
            send_sem=send.at[chunk, index],
            recv_sem=recv.at[chunk, index],
            device_id=(freq_to, 2 * half_to + parity),
            device_id_type=MESH,
        )

    def forward(chunk):
        swap(chunk).wait_recv()
        for freq_to in range(freq_devs):
            for half_to in range(pairs):
                summed[chunk, freq_to, half_to] = (
                    part[chunk, freq_to, half_to, parity] + mate_half[chunk, freq_to, half_to]
                )
        for index in range(len(others)):
            spread(chunk, index).start()

    def one_chunk(chunk, carry):
        def one_frequency(index, inner):
            flat[chunk, pl.ds(index, orbitals, stride=per_chunk), :] = last_step(
                chunk * per_chunk + index,
                freq_total,
                factor_ref,
                h_ref,
                sigma_ref,
                x_ref,
                last_left,
                last_right,
            )
            return inner

        lax.fori_loop(0, per_chunk, one_frequency, 0)

        @pl.when(chunk == 0)
        def _():
            pl.semaphore_wait(barrier, len(others) + 1)

        swap(chunk).start()

        @pl.when(chunk > 0)
        def _():
            forward(chunk - 1)

        return carry

    lax.fori_loop(0, chunks, one_chunk, 0)
    forward(chunks - 1)
    for chunk in range(chunks):
        total = summed[chunk, me, half]
        for index in range(len(others)):
            spread(chunk, index).wait_recv()
            total = total + landed[chunk, index]
        out_ref[chunk] = total
    for chunk in range(chunks):
        for index in range(len(others)):
            spread(chunk, index).wait_send()
        swap(chunk).wait_send()


def scatter(factors, hamiltonian, sigma, current, freq_devs, group_devs, chunks):
    k_local, orbitals, width = hamiltonian.shape
    freq_total = sigma.shape[0]
    pairs = group_devs // 2
    rows = orbitals * freq_total // (chunks * freq_devs * group_devs)
    peers = freq_devs * pairs - 1
    block = (rows, width)
    return pl.pallas_call(
        scatter_kernel,
        out_shape=jax.ShapeDtypeStruct((chunks,) + block, jnp.float32),
        in_specs=[VMEM] * 4,
        out_specs=VMEM,
        scratch_shapes=last_scratch(k_local, width)
        + [
            pltpu.VMEM((chunks, freq_devs, pairs, 2) + block, jnp.float32),
            pltpu.VMEM((chunks, freq_devs, pairs) + block, jnp.float32),
            pltpu.VMEM((chunks, freq_devs, pairs) + block, jnp.float32),
            pltpu.VMEM((chunks, peers) + block, jnp.float32),
            pltpu.SemaphoreType.DMA((chunks,)),
            pltpu.SemaphoreType.DMA((chunks,)),
            pltpu.SemaphoreType.DMA((chunks, peers)),
            pltpu.SemaphoreType.DMA((chunks, peers)),
        ],
        compiler_params=pltpu.CompilerParams(collective_id=1, has_side_effects=True),
        name="scatter",
    )(factors, hamiltonian, sigma, current)


def per_device(hamiltonian, self_energy, guess_factor, weights, counts):
    orbitals = hamiltonian.shape[1]
    per_freq = self_energy.shape[0]
    freq_devs = lax.axis_size("freq")
    group_devs = lax.axis_size("kgrp")
    freq_total = per_freq * freq_devs
    pair_block = orbitals * orbitals // (freq_devs * group_devs)
    pair_rows = pair_block // orbitals
    direct = pair_block % orbitals == 0 and group_devs % 2 == 0 and freq_devs % 2 == 0
    per_chunk = 8 // pair_rows if direct and 8 % pair_rows == 0 else freq_total
    direct = direct and freq_total % per_chunk == 0 and (pair_rows * per_chunk) % 8 == 0
    if direct:
        sigma, guess = gather(self_energy, guess_factor, freq_devs)
    else:
        sigma = lax.all_gather(self_energy, "freq", axis=0, tiled=True)
        guess = lax.all_gather(guess_factor, "freq", axis=0, tiled=True)
    current, factors = early_steps(counts, weights, hamiltonian, sigma, guess)
    if direct:
        chunks = freq_total // per_chunk
        own = scatter(factors, hamiltonian, sigma, current, freq_devs, group_devs, chunks)
        own = own.reshape(chunks, pair_rows, per_chunk, 2, orbitals)
        result = own.transpose(1, 4, 3, 0, 2)
    else:
        terms = local_sum(factors, hamiltonian, sigma, current)
        terms = terms.reshape(freq_total, orbitals, 2, orbitals).transpose(1, 3, 2, 0)
        terms = terms.reshape(orbitals * orbitals, 2 * freq_total)
        result = lax.psum_scatter(terms, ("freq", "kgrp"), scatter_dimension=0, tiled=True)
    return result.reshape(pair_block, 2 * freq_total)


def solution(mesh):
    return jax.shard_map(
        per_device,
        mesh=mesh,
        in_specs=(
            P(("freq", "kgrp"), None, None),
            P("freq", None, None),
            P("freq", None, None),
            P(),
            P(),
        ),
        out_specs=P(("freq", "kgrp"), None),
        check_vma=False,
    )
```

time: 59.2 us -> 55.7 us (0.941); the launches traced: 59.7 us -> 54.6 us
  Pallas kernels: 58.1 us -> 53.1 us
    pallas_call x2, Pallas kernels: 40.2 us -> 34.7 us  [the longest x1 23.8 us: scatter(): pl.pallas_call(scatter_kernel, out_shape=jax.ShapeDtypeStruct((chunks,) +...]
where the time goes in v2:
time: 55.7 us; the launch traced here: 54.6 us
  Pallas kernels  53.1 us (95%)
  local copies, waits for them, and re-layouts  1.51 us (3%)
    pallas_call x1, Pallas kernels, scatter(): pl.pallas_call(scatter_kernel, out_shape=jax.ShapeDtypeStruct((chunks,) +...  23.8 us
    pallas_call x1, Pallas kernels, gather(): pl.pallas_call(gather_kernel, out_shape=(full, full), in_specs=[VMEM, VME...  18.4 us
    pallas_call x1, Pallas kernels, early_steps(): pl.pallas_call(steps_kernel, out_shape=(jax.ShapeDtypeStruct((freq_total,...  10.9 us

profile of v2, /device:TPU:0, one launch (start us, length us, event | category | flops | bytes accessed | tf_op | source)
XLA Modules:
  0.0 54.6 jit_solution(14727313073276651826)
XLA Ops:
  0.0 18.4 %gather.1 = (f32[16,64,128]{2,1,0:T(8,128)}, f32[16,64,128]{2,1,0:T(8,128)}) custom-call(f32[2,64,128]{2,1,0:T(8,128)} %sigma_ref.1, f32[2,64,128]{2,1,0:T(8,128)} %guess_ref.1), custom_call_target="tpu_custom_call" | custom-call | tf_op jit(solution)/shard_map/gather/pallas_call | solution.py:283
  18.4 10.9 %early_steps.1 = (f32[16,8,64,128]{3,2,1,0:T(8,128)}, f32[8,128]{1,0:T(8,128)}) custom-call(s32[16]{0:T(128)} %counts.1, s32[256]{0:T(256)} %weights.1, f32[8,64,128]{2,1,0:T(8,128)} %h_ref.3, f32[16,64,128]{2,1,0:T(8,128)} %get-tuple-element.9.sigma_ref, f32[16,64,128]{2,1,0:T(8,128)} %get-tuple-element.10.guess_ref), custom_call_target="tpu_custom_call" | custom-call | tf_op jit(solution)/shard_map/early_steps/pallas_call | solution.py:124
  29.3 23.8 %scatter.1 = f32[4,8,128]{2,1,0:T(8,128)} custom-call(f32[8,128]{1,0:T(8,128)} %get-tuple-element.11.factor_ref, f32[8,64,128]{2,1,0:T(8,128)} %h_ref.3, f32[16,64,128]{2,1,0:T(8,128)} %get-tuple-element.9.sigma_ref, f32[16,8,64,128]{3,2,1,0:T(8,128)} %get-tuple-element.12.x_ref), custom_call_target="tpu_custom_call" | custom-call | tf_op jit(solution)/shard_map/scatter/pallas_call | solution.py:414
  53.1 0.8 %reshape.6 = f32[4,2,4,2,64]{4,3,2,1,0:T(2,128)S(1)} reshape(f32[4,8,128]{2,1,0:T(8,128)} %scatter.1) | data formatting | bytes 32768 | tf_op jit(solution)/shard_map/reshape | solution.py:455
  53.9 0.7 %reshape.7 = f32[128,32]{0,1:T(8,128)} reshape(f32[2,64,2,4,4]{1,0,4,3,2:T(2,128)S(1)} %copy.6) | data formatting | bytes 32768 | tf_op jit(solution)/shard_map/reshape | solution.py:462
  (1 shorter events, 0.0 us)

commit v3 on v2

--- a/solution.py
+++ b/solution.py
@@ -97,18 +97,24 @@
                 m_left[k] = left_operand(base - h_ref[k], orbitals, left)
 
             def newton_step(sweep, inner):
-                for k in range(k_local):
-                    current = x_ref[freq, k]
-                    product = jnp.dot(
-                        m_left[k], right_operand(current), preferred_element_type=jnp.float32
-                    )
-                    missing = eye_real - fold(product, orbitals, sign)
-                    product = jnp.dot(
-                        left_operand(current, orbitals, left),
-                        right_operand(missing),
+                products = [
+                    jnp.dot(
+                        m_left[k],
+                        right_operand(x_ref[freq, k]),
                         preferred_element_type=jnp.float32,
                     )
-                    x_ref[freq, k] = current + fold(product, orbitals, sign)
+                    for k in range(k_local)
+                ]
+                products = [
+                    jnp.dot(
+                        left_operand(x_ref[freq, k], orbitals, left),
+                        right_operand(eye_real - fold(products[k], orbitals, sign)),
+                        preferred_element_type=jnp.float32,
+                    )
+                    for k in range(k_local)
+                ]
+                for k in range(k_local):
+                    x_ref[freq, k] = x_ref[freq, k] + fold(products[k], orbitals, sign)
                 return inner
 
             lax.fori_loop(0, counts[freq] - 1, newton_step, 0)
@@ -141,19 +147,22 @@
     k_local, orbitals, width = h_ref.shape
     left, sign, eye_real, eye_imag = masks((orbitals, width))
     base = shifted(freq, freq_total, eye_real, eye_imag, sigma_ref[freq])
+    products = [
+        jnp.dot(
+            left_operand(base - h_ref[k], orbitals, left),
+            right_operand(x_ref[freq, k]),
+            preferred_element_type=jnp.float32,
+        )
+        for k in range(k_local)
+    ]
     total = jnp.zeros((orbitals, width), jnp.float32)
     for k in range(k_local):
-        current = x_ref[freq, k]
-        product = jnp.dot(
-            left_operand(base - h_ref[k], orbitals, left),
-            right_operand(current),
-            preferred_element_type=jnp.float32,
-        )
-        missing = eye_real - fold(product, orbitals, sign)
-        last_right[k * width : (k + 1) * width, :] = right_operand(missing)
-        weighted = current * factor_ref[k : k + 1, :]
+        weighted = x_ref[freq, k] * factor_ref[k : k + 1, :]
         last_left[:, k * width : (k + 1) * width] = left_operand(weighted, orbitals, left)
         total = total + weighted
+    for k in range(k_local):
+        missing = eye_real - fold(products[k], orbitals, sign)
+        last_right[k * width : (k + 1) * width, :] = right_operand(missing)
     product = jnp.dot(last_left[...], last_right[...], preferred_element_type=jnp.float32)
     return total + fold(product, orbitals, sign)
 

time: 55.7 us -> 56.4 us (1.013); the launches traced: 54.6 us -> 57.3 us
  Pallas kernels: 53.1 us -> 55.7 us
    pallas_call x1, Pallas kernels: 10.9 us -> 13.6 us  [early_steps(): pl.pallas_call(steps_kernel, out_shape=(jax.ShapeDtypeStruct((freq_total,...]
where the time goes in v3:
time: 56.4 us; the launch traced here: 57.3 us
  Pallas kernels  55.7 us (99%)
  local copies, waits for them, and re-layouts  1.51 us (3%)
    pallas_call x1, Pallas kernels, scatter(): pl.pallas_call(scatter_kernel, out_shape=jax.ShapeDtypeStruct((chunks,) +...  23.8 us
    pallas_call x1, Pallas kernels, gather(): pl.pallas_call(gather_kernel, out_shape=(full, full), in_specs=[VMEM, VME...  18.4 us
    pallas_call x1, Pallas kernels, early_steps(): pl.pallas_call(steps_kernel, out_shape=(jax.ShapeDtypeStruct((freq_total,...  13.6 us

profile of v3, /device:TPU:0, one launch (start us, length us, event | category | flops | bytes accessed | tf_op | source)
XLA Modules:
  0.0 57.3 jit_solution(14511574135870892442)
XLA Ops:
  0.0 18.4 %gather.1 = (f32[16,64,128]{2,1,0:T(8,128)}, f32[16,64,128]{2,1,0:T(8,128)}) custom-call(f32[2,64,128]{2,1,0:T(8,128)} %sigma_ref.1, f32[2,64,128]{2,1,0:T(8,128)} %guess_ref.1), custom_call_target="tpu_custom_call" | custom-call | tf_op jit(solution)/shard_map/gather/pallas_call | solution.py:292
  18.4 13.6 %early_steps.1 = (f32[16,8,64,128]{3,2,1,0:T(8,128)}, f32[8,128]{1,0:T(8,128)}) custom-call(s32[16]{0:T(128)} %counts.1, s32[256]{0:T(256)} %weights.1, f32[8,64,128]{2,1,0:T(8,128)} %h_ref.3, f32[16,64,128]{2,1,0:T(8,128)} %get-tuple-element.9.sigma_ref, f32[16,64,128]{2,1,0:T(8,128)} %get-tuple-element.10.guess_ref), custom_call_target="tpu_custom_call" | custom-call | tf_op jit(solution)/shard_map/early_steps/pallas_call | solution.py:130
  32.0 23.8 %scatter.1 = f32[4,8,128]{2,1,0:T(8,128)} custom-call(f32[8,128]{1,0:T(8,128)} %get-tuple-element.11.factor_ref, f32[8,64,128]{2,1,0:T(8,128)} %h_ref.3, f32[16,64,128]{2,1,0:T(8,128)} %get-tuple-element.9.sigma_ref, f32[16,8,64,128]{3,2,1,0:T(8,128)} %get-tuple-element.12.x_ref), custom_call_target="tpu_custom_call" | custom-call | tf_op jit(solution)/shard_map/scatter/pallas_call | solution.py:423
  55.7 0.8 %reshape.6 = f32[4,2,4,2,64]{4,3,2,1,0:T(2,128)S(1)} reshape(f32[4,8,128]{2,1,0:T(8,128)} %scatter.1) | data formatting | bytes 32768 | tf_op jit(solution)/shard_map/reshape | solution.py:464
  56.6 0.7 %reshape.7 = f32[128,32]{0,1:T(8,128)} reshape(f32[2,64,2,4,4]{1,0,4,3,2:T(2,128)S(1)} %copy.6) | data formatting | bytes 32768 | tf_op jit(solution)/shard_map/reshape | solution.py:471
  (1 shorter events, 0.0 us)

commit v4 on v3

--- a/solution.py
+++ b/solution.py
@@ -10,6 +10,7 @@
 
 chem_potential = 0.2
 MESH = pl.DeviceIdType.MESH
+GRANT = 32 * 1024 * 1024
 VMEM = pl.BlockSpec(memory_space=pltpu.VMEM)
 SMEM = pl.BlockSpec(memory_space=pltpu.SMEM)
 
@@ -139,6 +140,7 @@
             pltpu.VMEM((k_local, width, width), jnp.bfloat16),
             pltpu.VMEM((2, k_local, orbitals, width), jnp.float32),
         ],
+        compiler_params=pltpu.CompilerParams(vmem_limit_bytes=GRANT),
         name="early_steps",
     )(counts, weights, hamiltonian, sigma, guess)
 
@@ -295,7 +297,7 @@
         in_specs=[VMEM, VMEM],
         out_specs=(VMEM, VMEM),
         scratch_shapes=[pltpu.SemaphoreType.DMA((2,))] + [sems] * 6,
-        compiler_params=pltpu.CompilerParams(collective_id=0, has_side_effects=True),
+        compiler_params=pltpu.CompilerParams(collective_id=0, has_side_effects=True, vmem_limit_bytes=GRANT),
         name="gather",
     )(self_energy, guess_factor)
 
@@ -436,7 +438,7 @@
             pltpu.SemaphoreType.DMA((chunks, peers)),
             pltpu.SemaphoreType.DMA((chunks, peers)),
         ],
-        compiler_params=pltpu.CompilerParams(collective_id=1, has_side_effects=True),
+        compiler_params=pltpu.CompilerParams(collective_id=1, has_side_effects=True, vmem_limit_bytes=GRANT),
         name="scatter",
     )(factors, hamiltonian, sigma, current)
 

time: 56.4 us -> 51.8 us (0.918); the launches traced: 57.3 us -> 51.6 us
  Pallas kernels: 55.7 us -> 46.8 us
  local copies, waits for them, and re-layouts: 1.51 us -> 4.75 us
    pallas_call x1, Pallas kernels: 13.6 us -> 9.33 us  [early_steps(): pl.pallas_call(steps_kernel, out_shape=(jax.ShapeDtypeStruct((freq_total,...]
    unnamed x0 -> x10, local copies, waits for them, and re-layouts: none -> 3.96 us
    pallas_call x1, Pallas kernels: 23.8 us -> 20.9 us  [scatter(): pl.pallas_call(scatter_kernel, out_shape=jax.ShapeDtypeStruct((chunks,) +...]
    pallas_call x1, Pallas kernels: 18.4 us -> 16.5 us  [gather(): pl.pallas_call(gather_kernel, out_shape=(full, full), in_specs=[VMEM, VME...]
    reshape x1, local copies, waits for them, and re-layouts: 0.8 us -> 0.09 us  [per_device(): own = own.reshape(chunks, pair_rows, per_chunk, 2, orbitals)]
where the time goes in v4:
time: 51.8 us; the launch traced here: 51.6 us
  Pallas kernels  46.8 us (90%)
  local copies, waits for them, and re-layouts  4.75 us (9%)
    pallas_call x1, Pallas kernels, scatter(): pl.pallas_call(scatter_kernel, out_shape=jax.ShapeDtypeStruct((chunks,) +...  20.9 us
    pallas_call x1, Pallas kernels, gather(): pl.pallas_call(gather_kernel, out_shape=(full, full), in_specs=[VMEM, VME...  16.5 us
    pallas_call x1, Pallas kernels, early_steps(): pl.pallas_call(steps_kernel, out_shape=(jax.ShapeDtypeStruct((freq_total,...  9.33 us
    unnamed x10, local copies, waits for them, and re-layouts  3.96 us

profile of v4, /device:TPU:0, one launch (start us, length us, event | category | flops | bytes accessed | tf_op | source)
XLA Modules:
  0.0 51.6 jit_solution(647976212597292162)
XLA Ops:
  0.0 0.0 copy-start.1
  0.0 0.8 %copy-done.1 = f32[2,64,128]{2,1,0:T(8,128)S(1)} copy-done((f32[2,64,128]{2,1,0:T(8,128)S(1)}, f32[2,64,128]{2,1,0:T(8,128)}, u32[]{:S(2)}) %copy-start.1) | copy-done | bytes 65560
  0.8 0.0 copy-start.2
  0.8 0.8 %copy-done.2 = f32[2,64,128]{2,1,0:T(8,128)S(1)} copy-done((f32[2,64,128]{2,1,0:T(8,128)S(1)}, f32[2,64,128]{2,1,0:T(8,128)}, u32[]{:S(2)}) %copy-start.2) | copy-done | bytes 65560
  1.7 16.5 %gather.1 = (f32[16,64,128]{2,1,0:T(8,128)S(1)}, f32[16,64,128]{2,1,0:T(8,128)S(1)}) custom-call(f32[2,64,128]{2,1,0:T(8,128)S(1)} %copy-done.1, f32[2,64,128]{2,1,0:T(8,128)S(1)} %copy-done.2), custom_call_target="tpu_custom_call" | custom-call | tf_op jit(solution)/shard_map/gather/pallas_call | solution.py:294
  18.2 0.0 copy-start
  18.2 0.9 %copy-done = f32[8,64,128]{2,1,0:T(8,128)S(1)} copy-done((f32[8,64,128]{2,1,0:T(8,128)S(1)}, f32[8,64,128]{2,1,0:T(8,128)}, u32[]{:S(2)}) %copy-start) | copy-done | bytes 262168
  19.2 0.0 copy-start.3
  19.2 0.7 %copy-done.3 = s32[256]{0:T(256)S(1)} copy-done((s32[256]{0:T(256)S(1)}, s32[256]{0:T(256)}, u32[]{:S(2)}) %copy-start.3) | copy-done | bytes 1048
  19.9 0.0 copy-start.4
  19.9 0.7 %copy-done.4 = s32[16]{0:T(128)S(1)} copy-done((s32[16]{0:T(128)S(1)}, s32[16]{0:T(128)}, u32[]{:S(2)}) %copy-start.4) | copy-done | bytes 88
  20.5 9.3 %early_steps.1 = (f32[16,8,64,128]{3,2,1,0:T(8,128)S(1)}, f32[8,128]{1,0:T(8,128)S(1)}) custom-call(s32[16]{0:T(128)S(1)} %copy-done.4, s32[256]{0:T(256)S(1)} %copy-done.3, f32[8,64,128]{2,1,0:T(8,128)S(1)} %copy-done, f32[16,64,128]{2,1,0:T(8,128)S(1)} %get-tuple-element.9.sigma_ref, f32[16,64,128]{2,1,0:T(8,128)S(1)} %get-tuple-element.10.guess_ref), custom_call_target="tpu_custom_call" | custom-call | tf_op jit(solution)/shard_map/early_steps/pallas_call | solution.py:131
  29.9 20.9 %scatter.1 = f32[4,8,128]{2,1,0:T(8,128)S(1)} custom-call(f32[8,128]{1,0:T(8,128)S(1)} %get-tuple-element.11.factor_ref, f32[8,64,128]{2,1,0:T(8,128)S(1)} %copy-done, f32[16,64,128]{2,1,0:T(8,128)S(1)} %get-tuple-element.9.sigma_ref, f32[16,8,64,128]{3,2,1,0:T(8,128)S(1)} %get-tuple-element.12.x_ref), custom_call_target="tpu_custom_call" | custom-call | tf_op jit(solution)/shard_map/scatter/pallas_call | solution.py:425
  50.8 0.1 reshape.6
  50.9 0.7 %reshape.7 = f32[128,32]{0,1:T(8,128)} reshape(f32[2,64,2,4,4]{1,0,4,3,2:T(2,128)S(1)} %copy.6) | data formatting | bytes 32768 | tf_op jit(solution)/shard_map/reshape | solution.py:473
  (1 shorter events, 0.0 us)
Async XLA Ops:
  0.0 0.8 %copy-start.1 = (f32[2,64,128]{2,1,0:T(8,128)S(1)}, f32[2,64,128]{2,1,0:T(8,128)}, u32[]{:S(2)}) copy-start(f32[2,64,128]{2,1,0:T(8,128)} %sigma_ref.1) | copy-start | bytes 196612
  0.8 0.8 %copy-start.2 = (f32[2,64,128]{2,1,0:T(8,128)S(1)}, f32[2,64,128]{2,1,0:T(8,128)}, u32[]{:S(2)}) copy-start(f32[2,64,128]{2,1,0:T(8,128)} %guess_ref.1) | copy-start | bytes 196612
  18.2 1.0 %copy-start = (f32[8,64,128]{2,1,0:T(8,128)S(1)}, f32[8,64,128]{2,1,0:T(8,128)}, u32[]{:S(2)}) copy-start(f32[8,64,128]{2,1,0:T(8,128)} %h_ref.3) | copy-start | bytes 786436
  19.2 0.7 %copy-start.3 = (s32[256]{0:T(256)S(1)}, s32[256]{0:T(256)}, u32[]{:S(2)}) copy-start(s32[256]{0:T(256)} %weights.1) | copy-start | bytes 3076
  19.9 0.7 %copy-start.4 = (s32[16]{0:T(128)S(1)}, s32[16]{0:T(128)}, u32[]{:S(2)}) copy-start(s32[16]{0:T(128)} %counts.1) | copy-start | bytes 196
